TPU v7x, 8 devices: a whole 2x2x1 slice. The times are simulated.
8 devices in a mesh: replica: 2 (over z, y), data: 4 (over x, core).
Axes of the slice: x: 2, y: 2, z: 1, core: 2. Of those that a mesh axis runs over, the one named last changes fastest.
Arguments:
- inp_rows: bfloat16 [8192, 1536], P(('replica', 'data'))
- out_grad: bfloat16 [8192, 1536], P(('replica', 'data'))
- w_up: bfloat16 [2, 1536, 8960], replicated
- w_down: bfloat16 [2, 8960, 1536], replicated
- master_up: float32 [2, 1536, 8960], P(None, 'data')
- master_down: float32 [2, 8960, 1536], P(None, 'data')
- mom_up: float32 [2, 1536, 8960], P(None, 'data')
- mom_down: float32 [2, 8960, 1536], P(None, 'data')
- var_up: float32 [2, 1536, 8960], P(None, 'data')
- var_down: float32 [2, 8960, 1536], P(None, 'data')
- clip_norm: float32 [], replicated
Outputs:
- output 1: bfloat16 [2, 1536, 8960], replicated
- output 2: bfloat16 [2, 8960, 1536], replicated
- output 3: float32 [2, 1536, 8960], P(None, 'data')
- output 4: float32 [2, 8960, 1536], P(None, 'data')
- output 5: float32 [2, 1536, 8960], P(None, 'data')
- output 6: float32 [2, 8960, 1536], P(None, 'data')
- output 7: float32 [2, 1536, 8960], P(None, 'data')
- output 8: float32 [2, 8960, 1536], P(None, 'data')
- output 9: float32 [], replicated
All inputs are finite; a program needn't handle non-finite values.
Results may differ from a plain program's by a relative error of at most 0.00917307.
Values are sent between devices in bfloat16 or wider.
A program may use at most 2.25 GiB of HBM per device.

v0:
```python
import jax
import jax.numpy as jnp
from jax import lax
from jax.sharding import PartitionSpec as P

BETA1 = 0.9
BETA2 = 0.95
ADAM_EPS = 1e-8
LEARN_RATE = 5e-3
NORM_EPS = 1e-6
STEP = 10
BIAS_ONE = 1.0 - BETA1 ** STEP
BIAS_TWO = 1.0 - BETA2 ** STEP


def gelu_value(pre_act):
    return pre_act * (0.5 + 0.5 * lax.erf(pre_act * 0.7071067811865476))


def gelu_slope(pre_act):
    return 0.5 + 0.5 * lax.erf(pre_act * 0.7071067811865476) + pre_act * jnp.exp(-0.5 * pre_act * pre_act) * 0.3989422804014327


def local_backward(inp_rows, out_grad, w_up, w_down):
    up_one = w_up[0]
    up_two = w_up[1]
    down_one = w_down[0]
    down_two = w_down[1]
    pre_one = jnp.dot(inp_rows, up_one, preferred_element_type=jnp.float32).astype(jnp.bfloat16)
    act_one = gelu_value(pre_one.astype(jnp.float32)).astype(jnp.bfloat16)
    mid_rows = jnp.dot(act_one, down_one, preferred_element_type=jnp.float32).astype(jnp.bfloat16)
    pre_two = jnp.dot(mid_rows, up_two, preferred_element_type=jnp.float32).astype(jnp.bfloat16)
    act_two = gelu_value(pre_two.astype(jnp.float32)).astype(jnp.bfloat16)
    grad_down2 = jnp.einsum('bf,bd->fd', act_two, out_grad, preferred_element_type=jnp.float32)
    dact_two = jnp.einsum('bd,fd->bf', out_grad, down_two, preferred_element_type=jnp.float32).astype(jnp.bfloat16)
    dpre_two = (dact_two.astype(jnp.float32) * gelu_slope(pre_two.astype(jnp.float32))).astype(jnp.bfloat16)
    grad_up2 = jnp.einsum('bd,bf->df', mid_rows, dpre_two, preferred_element_type=jnp.float32)
    dmid_rows = jnp.einsum('bf,df->bd', dpre_two, up_two, preferred_element_type=jnp.float32).astype(jnp.bfloat16)
    grad_down1 = jnp.einsum('bf,bd->fd', act_one, dmid_rows, preferred_element_type=jnp.float32)
    dact_one = jnp.einsum('bd,fd->bf', dmid_rows, down_one, preferred_element_type=jnp.float32).astype(jnp.bfloat16)
    dpre_one = (dact_one.astype(jnp.float32) * gelu_slope(pre_one.astype(jnp.float32))).astype(jnp.bfloat16)
    grad_up1 = jnp.einsum('bd,bf->df', inp_rows, dpre_one, preferred_element_type=jnp.float32)
    return grad_down2, grad_up2, grad_down1, grad_up1


def adam_update(grad_vals, master_vals, mom_vals, var_vals, clip_scale):
    new_mom = BETA1 * mom_vals + (1.0 - BETA1) * clip_scale * grad_vals
    new_var = BETA2 * var_vals + (1.0 - BETA2) * (clip_scale * clip_scale) * (grad_vals * grad_vals)
    new_master = master_vals - LEARN_RATE * (new_mom / BIAS_ONE) / (jnp.sqrt(new_var / BIAS_TWO) + ADAM_EPS)
    return new_master, new_mom, new_var


def solution(mesh):
    total_devices = mesh.shape['replica'] * mesh.shape['data']
    batch_spec = P(('replica', 'data'), None)
    whole_spec = P()
    shard_spec = P(None, 'data', None)

    def device_step(inp_rows, out_grad, w_up, w_down, master_up, master_down, mom_up, mom_down, var_up, var_down, clip_norm):
        grad_down2, grad_up2, grad_down1, grad_up1 = local_backward(inp_rows, out_grad, w_up, w_down)
        shard_down2 = lax.psum_scatter(grad_down2, 'data', scatter_dimension=0, tiled=True)
        shard_up2 = lax.psum_scatter(grad_up2, 'data', scatter_dimension=0, tiled=True)
        shard_down1 = lax.psum_scatter(grad_down1, 'data', scatter_dimension=0, tiled=True)
        shard_up1 = lax.psum_scatter(grad_up1, 'data', scatter_dimension=0, tiled=True)
        grad_up = lax.psum(jnp.stack([shard_up1, shard_up2]), 'replica') / total_devices
        grad_down = lax.psum(jnp.stack([shard_down1, shard_down2]), 'replica') / total_devices
        local_sq = jnp.sum(grad_up * grad_up) + jnp.sum(grad_down * grad_down)
        grad_norm = jnp.sqrt(lax.psum(local_sq, 'data'))
        clip_scale = jnp.minimum(1.0, clip_norm / (grad_norm + NORM_EPS))
        master_up_new, mom_up_new, var_up_new = adam_update(grad_up, master_up, mom_up, var_up, clip_scale)
        master_down_new, mom_down_new, var_down_new = adam_update(grad_down, master_down, mom_down, var_down, clip_scale)
        w_up_new = lax.all_gather(master_up_new.astype(jnp.bfloat16), 'data', axis=1, tiled=True)
        w_down_new = lax.all_gather(master_down_new.astype(jnp.bfloat16), 'data', axis=1, tiled=True)
        return (w_up_new, w_down_new, master_up_new, master_down_new, mom_up_new, mom_down_new, var_up_new, var_down_new, grad_norm)

    return jax.shard_map(device_step, mesh=mesh, in_specs=(batch_spec, batch_spec, whole_spec, whole_spec, shard_spec, shard_spec, shard_spec, shard_spec, shard_spec, shard_spec, whole_spec), out_specs=(whole_spec, whole_spec, shard_spec, shard_spec, shard_spec, shard_spec, shard_spec, shard_spec, whole_spec), check_vma=False)
```

profile of v0, /device:TPU:0, one launch (start us, length us, event | category | flops | bytes accessed | tf_op | source)
XLA Modules:
  0.0 3692.1 jit_solution(3654310027155007327)
XLA Ops:
  7.2 0.0 reduce-scatter.7.cloned.1.call-start
  7.2 1.8 copy-done
  9.1 34.9 fusion.50
  44.0 33.4 fusion.56
  77.4 35.3 fusion.53
  112.7 41.6 %fusion.16 = bf16[1024,8960]{1,0:T(8,128)(2,1)} fusion(bf16[1024,8960]{1,0:T(8,128)(2,1)} %fusion.53, bf16[1024,1536]{1,0:T(8,128)(2,1)S(1)} %copy-done.3, bf16[2,8960,1536]{2,1,0:T(8,128)(2,1)} %param.14), kind=kOutput, calls=%fused_computation.27 | convolution fusion | flops 28304998400 | bytes 67371008 | tf_op jit(solution)/shard_map/bd,fd->bf/dot_general | solution.py:35
  154.3 36.3 fusion.73
  190.6 0.0 reduce-scatter.7.cloned.1.call-update
  190.7 0.0 reduce-scatter.5.cloned.1.call-start
  190.7 39.0 %fusion.59 = bf16[1024,1536]{1,0:T(8,128)(2,1)} fusion(bf16[1024,8960]{1,0:T(8,128)(2,1)} %fusion.16, bf16[2,1536,8960]{2,1,0:T(8,128)(2,1)} %param.13), kind=kOutput, calls=%fused_computation.66 | convolution fusion | flops 28187295744 | bytes 49020928 | tf_op jit(solution)/shard_map/bf,df->bd/dot_general | solution.py:38
  229.8 48.9 %fusion.102 = bf16[1024,8960]{1,0:T(8,128)(2,1)S(1)} fusion(bf16[1024,8960]{1,0:T(8,128)(2,1)} %fusion.50, bf16[1024,1536]{1,0:T(8,128)(2,1)} %fusion.59, bf16[2,8960,1536]{2,1,0:T(8,128)(2,1)} %param.14), kind=kOutput, calls=%fused_computation.19.clone.clone.1 | convolution fusion | flops 28304998400 | bytes 67371008 | tf_op jit(solution)/shard_map/bd,fd->bf/dot_general | solution.py:40
  278.7 34.4 convolution_bitcast_fusion
  313.1 0.0 reduce-scatter.5.cloned.1.call-update
  313.1 0.0 reduce-scatter.9.cloned.1.call-start
  313.2 1.8 copy-done.5
  315.0 36.4 fusion.64
  351.4 0.0 reduce-scatter.9.cloned.1.call-update
  351.4 0.0 reduce-scatter.11.cloned.1.call-start
  351.5 1.8 copy-done.4
  353.3 36.6 fusion.38
  389.9 0.0 all-reduce.3.cloned.1.call-start
  390.0 159.0 %reduce-scatter.7.cloned.1.call-done = f32[384,8960]{0,1:T(8,128)} async-done(((f32[1536,8960]{0,1:T(8,128)}), f32[384,8960]{0,1:T(8,128)}) %reduce-scatter.7.cloned.1.call-update) | async-done | bytes 13762576 | tf_op jit(solution)/shard_map/reduce_scatter | solution.py:62
  549.0 358.5 %reduce-scatter.5.cloned.1.call-done = f32[384,8960]{0,1:T(8,128)} async-done(((f32[1536,8960]{0,1:T(8,128)}), f32[384,8960]{0,1:T(8,128)}) %reduce-scatter.5.cloned.1.call-update) | async-done | bytes 13762576 | tf_op jit(solution)/shard_map/reduce_scatter | solution.py:64
  907.5 23.4 pad_maximum_fusion
  930.8 351.6 %reduce-scatter.9.cloned.1.call-done = f32[2240,1536]{1,0:T(8,128)} async-done(((f32[8960,1536]{1,0:T(8,128)}), f32[2240,1536]{1,0:T(8,128)}) %reduce-scatter.9.cloned.1.call-update) | async-done | bytes 13762576 | tf_op jit(solution)/shard_map/reduce_scatter | solution.py:63
  1282.5 374.9 %reduce-scatter.11.cloned.1.call-done = f32[2240,1536]{1,0:T(8,128)} async-done(((f32[8960,1536]{1,0:T(8,128)}), f32[2240,1536]{1,0:T(8,128)}) %reduce-scatter.11.cloned.1.call-update) | async-done | bytes 13762576 | tf_op jit(solution)/shard_map/reduce_scatter | solution.py:61
  1657.4 20.5 pad_maximum_fusion.1
  1677.9 0.0 all-gather.3.cloned.1.call-start
  1678.6 27.1 copy.23
  1705.7 27.4 copy.20
  1733.0 1137.9 %all-reduce.3.cloned.1.call-done = (f32[2,384,8960]{1,2,0:T(8,128)}, f32[2,2240,1536]{2,1,0:T(8,128)}) async-done(((f32[2,384,8960]{1,2,0:T(8,128)}, f32[2,2240,1536]{2,1,0:T(8,128)}), (f32[2,384,8960]{1,2,0:T(8,128)}, f32[2,2240,1536]{2,1,0:T(8,128)})) %all-reduce.3.cloned.1.call-update) | async-done | bytes 55050256 | tf_op jit(solution)/shard_map/psum | solution.py:65
  2870.9 14.4 fusion.33
  2885.3 2.3 copy-done.2
  2887.7 7.7 fusion.32
  2896.7 26.8 copy.22
  2923.5 7.1 psum.23
  2931.3 69.1 %fusion.72 = (bf16[2,384,8960]{1,2,0:T(8,128)(2,1)}, f32[2,384,8960]{1,2,0:T(8,128)}, f32[2,384,8960]{1,2,0:T(8,128)}, f32[2,384,8960]{1,2,0:T(8,128)}) fusion(f32[2,384,8960]{1,2,0:T(8,128)} %copy.23, f32[2,384,8960]{1,2,0:T(8,128)} %get-tuple-element.18, f32[]{:T(128)S(6)} %mul.152, f32[2,384,8960]{1,2,0:T(8,128)} %copy.20, f32[]{:T(128)S(6)} %mul.160, ...), kind=kLoop, calls=%fused_computation.71 | loop fusion | flops 96337920 | bytes 206438400 | tf_op jit(solution)/shard_map/convert_element_type | solution.py:72
  3000.5 0.0 all-gather.3.cloned.1.call-update
  3000.5 0.0 all-gather.5.cloned.1.call-start
  3000.5 77.4 %fusion.71 = (bf16[2,2240,1536]{2,1,0:T(8,128)(2,1)}, f32[2,2240,1536]{2,1,0:T(8,128)}, f32[2,2240,1536]{2,1,0:T(8,128)}, f32[2,2240,1536]{2,1,0:T(8,128)}) fusion(f32[2,2240,1536]{2,1,0:T(8,128)} %param.16, f32[2,2240,1536]{2,1,0:T(8,128)} %get-tuple-element.19, f32[]{:T(128)S(6)} %mul.152, f32[2,2240,1536]{2,1,0:T(8,128)} %param.18, f32[]{:T(128)S(6)} %mul.160, ...), kind=kLoop, calls=%fused_computation.70 | loop fusion | flops 96337920 | bytes 206438400 | tf_op jit(solution)/shard_map/convert_element_type | solution.py:73
  3078.0 27.3 copy.25
  3105.3 27.4 copy.26
  3132.7 27.3 copy.27
  3160.0 162.2 %all-gather.3.cloned.1.call-done = bf16[2,1536,8960]{1,2,0:T(8,128)(2,1)} async-done(((bf16[2,384,8960]{1,2,0:T(8,128)(2,1)}), bf16[2,1536,8960]{1,2,0:T(8,128)(2,1)}) %all-gather.3.cloned.1.call-update) | async-done | bytes 55050256 | tf_op jit(solution)/shard_map/all_gather | solution.py:72
  3322.3 67.4 %copy.24 = bf16[2,1536,8960]{2,1,0:T(8,128)(2,1)} copy(bf16[2,1536,8960]{1,2,0:T(8,128)(2,1)} %all-gather.3.cloned.1.call-done) | data formatting | bytes 110100480
  3389.7 256.0 %all-gather.5.cloned.1.call-done = bf16[2,8960,1536]{2,1,0:T(8,128)(2,1)} async-done(((bf16[2,2240,1536]{2,1,0:T(8,128)(2,1)}), bf16[2,8960,1536]{2,1,0:T(8,128)(2,1)}) %all-gather.5.cloned.1.call-update) | async-done | bytes 55050256 | tf_op jit(solution)/shard_map/all_gather | solution.py:73
  3645.7 37.0 %copy.33 = bf16[2,8960,1536]{2,1,0:T(8,128)(2,1)} copy(bf16[2,8960,1536]{2,1,0:T(8,128)(2,1)} %all-gather.5.cloned.1.call-done) | data formatting | bytes 110100480
  3682.7 1.0 copy-done.1
  (10 shorter events, 0.1 us)
Async XLA Ops:
  7.2 1.9 copy-start
  7.2 541.8 %reduce-scatter.7.cloned.1.call-start = ((), (), s32[]{:S(2)}) async-start(), calls=%async_computation.5 | async-start | bytes 68812800 | tf_op jit(solution)/shard_map/reduce_scatter | solution.py:62
  77.4 35.3 copy-start.3
  190.7 716.8 %reduce-scatter.5.cloned.1.call-start = ((), (), s32[]{:S(2)}) async-start(), calls=%async_computation.4 | async-start | bytes 68812800 | tf_op jit(solution)/shard_map/reduce_scatter | solution.py:64
  313.1 1.9 copy-start.5
  313.1 969.4 %reduce-scatter.9.cloned.1.call-start = ((), (), s32[]{:S(2)}) async-start(), calls=%async_computation.6 | async-start | bytes 68812800 | tf_op jit(solution)/shard_map/reduce_scatter | solution.py:63
  351.4 1.9 copy-start.4
  351.4 1306.0 %reduce-scatter.11.cloned.1.call-start = ((), (), s32[]{:S(2)}) async-start(), calls=%async_computation.7 | async-start | bytes 68812800 | tf_op jit(solution)/shard_map/reduce_scatter | solution.py:61
  389.9 2481.0 %all-reduce.3.cloned.1.call-start = ((), (), s32[]{:S(2)}) async-start(), calls=%async_computation.10 | async-start | bytes 110100480 | tf_op jit(solution)/shard_map/psum | solution.py:65
  1677.9 1644.4 %all-gather.3.cloned.1.call-start = ((), (), s32[]{:S(2)}) async-start(), calls=%async_computation.8 | async-start | bytes 68812800 | tf_op jit(solution)/shard_map/all_gather | solution.py:72
  2870.9 16.7 copy-start.2
  3000.5 645.2 %all-gather.5.cloned.1.call-start = ((), (), s32[]{:S(2)}) async-start(), calls=%async_computation.9 | async-start | bytes 68812800 | tf_op jit(solution)/shard_map/all_gather | solution.py:73
  3645.7 38.0 %copy-start.1 = (bf16[1024,1536]{1,0:T(8,128)(2,1)S(1)}, bf16[1024,1536]{1,0:T(8,128)(2,1)}, u32[]{:S(2)}) copy-start(bf16[1024,1536]{1,0:T(8,128)(2,1)} %param.11) | copy-start | bytes 9437188
Sparse Core Ops, SparseCore 0:
  190.8 358.1 reduce-scatter.6
  552.1 355.3 reduce-scatter.4
  910.0 372.4 reduce-scatter.8
  1284.9 372.4 reduce-scatter.10
  1678.0 1192.8 all-reduce.2
  3000.6 321.5 all-gather.2
  3323.8 321.8 all-gather.4
where the time goes:
time: 3700 us; the launch traced here: 3690 us
  waiting for transfers between devices  2800 us (76%)
  matrix products  377 us (10%)
  local copies, waits for them, and re-layouts  277 us (7%)
  other arithmetic  212 us (6%)
    psum x1, waiting for transfers between devices, device_step(): lax.psum(jnp.stack([shard_up1, shard_up2]), 'replica') / total_devices  1140 us
    reduce_scatter x1, waiting for transfers between devices, device_step(): lax.psum_scatter(grad_down2, 'data', scatter_dimension=0, tiled=True)  375 us
    reduce_scatter x1, waiting for transfers between devices, device_step(): lax.psum_scatter(grad_up1, 'data', scatter_dimension=0, tiled=True)  358 us
    reduce_scatter x1, waiting for transfers between devices, device_step(): lax.psum_scatter(grad_down1, 'data', scatter_dimension=0, tiled=True)  352 us
    unnamed x20, local copies, waits for them, and re-layouts  277 us
    all_gather x1, waiting for transfers between devices, device_step(): lax.all_gather(master_down_new.astype(jnp.bfloat16), 'data', axis=1, tile...  256 us
    all_gather x1, waiting for transfers between devices, device_step(): lax.all_gather(master_up_new.astype(jnp.bfloat16), 'data', axis=1, tiled=...  162 us
    reduce_scatter x1, waiting for transfers between devices, device_step(): lax.psum_scatter(grad_up2, 'data', scatter_dimension=0, tiled=True)  159 us
  transfers between devices with their start and end apart: 7, of which 7 were waited for; matrix products, arithmetic and copies ran while one was open for 14% of the time, Pallas kernels for 0%

commit v1 on v0

v1 whole, which is shorter than its diff:
```python
import jax
import jax.numpy as jnp
from jax import lax
from jax.sharding import PartitionSpec as P


BETA1 = 0.9
BETA2 = 0.95
ADAM_EPS = 1e-8
LEARN_RATE = 5e-3
NORM_EPS = 1e-6
STEP = 10
BIAS_ONE = 1.0 - BETA1 ** STEP
BIAS_TWO = 1.0 - BETA2 ** STEP
F32 = jnp.float32
BF16 = jnp.bfloat16
CHUNKS = {'d2': 2, 'u2': 2, 'd1': 2, 'u1': 4}


def gelu_value(pre_act):
    return pre_act * (0.5 + 0.5 * lax.erf(pre_act * 0.7071067811865476))


def gelu_slope(pre_act):
    return 0.5 + 0.5 * lax.erf(pre_act * 0.7071067811865476) + pre_act * jnp.exp(-0.5 * pre_act * pre_act) * 0.3989422804014327


def mul(left, right, left_dim, right_dim):
    return lax.dot_general(left, right, (((left_dim,), (right_dim,)), ((), ())), preferred_element_type=F32)


def act(pre):
    return gelu_value(pre.astype(F32)).astype(BF16)


def back(dact, pre):
    return (dact.astype(F32) * gelu_slope(pre.astype(F32))).astype(BF16)


def adam_parts(grad_vals, mom_vals, var_vals, clip_scale):
    new_mom = BETA1 * mom_vals + (1.0 - BETA1) * clip_scale * grad_vals
    new_var = BETA2 * var_vals + (1.0 - BETA2) * (clip_scale * clip_scale) * (grad_vals * grad_vals)
    return new_mom, new_var


def adam_master(new_mom, new_var, master_vals):
    return master_vals - LEARN_RATE * (new_mom / BIAS_ONE) / (jnp.sqrt(new_var / BIAS_TWO) + ADAM_EPS)


def solution(mesh):
    replicas, shards = mesh.shape['replica'], mesh.shape['data']
    total_devices = replicas * shards
    batch_spec = P(('replica', 'data'), None)
    whole_spec = P()
    shard_spec = P(None, 'data', None)
    along_x = [(i, i ^ 2) for i in range(shards)]
    along_core = [(i, i ^ 1) for i in range(shards)]
    along_y = [(i, i ^ 1) for i in range(replicas)]

    def swap_x(val):
        return lax.ppermute(val, 'data', along_x)

    def swap_c(val):
        return lax.ppermute(val, 'data', along_core)

    def swap_y(val):
        return lax.ppermute(val, 'replica', along_y)

    def device_step(inp_rows, out_grad, w_up, w_down, master_up, master_down, mom_up, mom_down, var_up, var_down, clip_norm):
        rep = lax.axis_index('replica')
        dat = lax.axis_index('data')
        own_x, own_c = dat // 2, dat % 2
        dim, hid = w_up.shape[1], w_up.shape[2]
        up_rows, down_rows = dim // shards, hid // shards
        half_dim, half_hid = dim // 2, hid // 2

        inp_far = swap_y(inp_rows)
        grad_far = swap_y(out_grad)
        up_one, up_two = w_up[0], w_up[1]
        down_one, down_two = w_down[0], w_down[1]

        pre_near = mul(up_one, inp_rows, 0, 1).astype(BF16)
        act_near = lax.optimization_barrier(act(pre_near))
        mid_near = mul(act_near, down_one, 0, 0).astype(BF16)
        pre_far = mul(up_one, inp_far, 0, 1).astype(BF16)
        act_far = lax.optimization_barrier(act(pre_far))
        mid_far = mul(act_far, down_one, 0, 0).astype(BF16)
        mid_all = jnp.concatenate([mid_near, mid_far], axis=0)
        pre_two = mul(up_two, mid_all, 0, 1).astype(BF16)
        act_two = act(pre_two)
        dy_all = jnp.concatenate([out_grad, grad_far], axis=0)

        pieces = {}

        def reduce_piece(make, name, axis, size):
            far_x, far_c = 1 - own_x, 1 - own_c
            unit = 128 if axis else 16
            count = CHUNKS[name]
            ends = [unit * ((size // unit * (idx + 1) + count - 1) // count) for idx in range(count)]
            spans = list(zip([0] + ends[:-1], [end - start for start, end in zip([0] + ends[:-1], ends)]))

            def summed(x_idx):
                sent = []
                for span in spans:
                    part = make(x_idx, far_c, *span)
                    sent.append(swap_c(part))
                sums = []
                for idx, span in enumerate(spans):
                    sums.append(make(x_idx, own_c, *span) + sent[idx])
                return sums

            sum_far = summed(far_x)
            from_x = []
            for val in sum_far:
                from_x.append(swap_x(val))
            sum_own = summed(own_x)
            near_parts, far_parts, squares = [], [], 0.0
            for idx, val in enumerate(sum_own):
                came = from_x[idx]
                if near_parts:
                    came, near_parts[-1] = lax.optimization_barrier((came, near_parts[-1]))
                grad = (val + came) / total_devices
                squares = squares + jnp.sum(grad * grad)
                near_parts.append(grad)
                far_parts.append(swap_y(grad))
            pieces[name] = (jnp.concatenate(near_parts, axis=axis), squares, near_parts, far_parts, spans, axis)

        def down_maker(acts, grads):
            def make(x_idx, c_idx, start, size):
                total = None
                for act_t, grad in zip(acts, grads):
                    lhs = lax.dynamic_slice(act_t, ((2 * x_idx + c_idx) * down_rows + start, 0), (size, act_t.shape[1]))
                    rhs = lax.dynamic_slice(grad, (0, rep * half_dim), (grad.shape[0], half_dim))
                    part = mul(lhs, rhs, 1, 0)
                    total = part if total is None else total + part
                return total

            return make

        def up_maker(inps, dpres):
            def make(x_idx, c_idx, start, size):
                total = None
                for inp, dpre in zip(inps, dpres):
                    lhs = lax.dynamic_slice(inp, (0, (2 * x_idx + c_idx) * up_rows), (inp.shape[0], up_rows))
                    rhs = lax.dynamic_slice(dpre, (rep * half_hid + start, 0), (size, dpre.shape[1]))
                    part = mul(lhs, rhs, 0, 1)
                    total = part if total is None else total + part
                return total

            return make

        reduce_piece(down_maker([act_two], [dy_all]), 'd2', 0, down_rows)
        dact_two = mul(down_two, dy_all, 1, 1).astype(BF16)
        dpre_two = back(dact_two, pre_two)
        reduce_piece(up_maker([mid_all], [dpre_two]), 'u2', 1, half_hid)
        dmid = mul(dpre_two, up_two, 0, 1).astype(BF16)
        dmid_near, dmid_far = lax.optimization_barrier((dmid[:inp_rows.shape[0]], dmid[inp_rows.shape[0]:]))
        reduce_piece(down_maker([act_near, act_far], [dmid_near, dmid_far]), 'd1', 0, down_rows)
        dpre_near = back(mul(down_one, dmid_near, 1, 1).astype(BF16), pre_near)
        dpre_far = back(mul(down_one, dmid_far, 1, 1).astype(BF16), pre_far)
        reduce_piece(up_maker([inp_rows, inp_far], [dpre_near, dpre_far]), 'u1', 1, half_hid)

        local_sq = sum(pieces[name][1] for name in ('d2', 'u2', 'd1', 'u1'))
        grad_norm = jnp.sqrt(lax.psum(local_sq, ('replica', 'data')))
        clip_scale = jnp.minimum(1.0, clip_norm / (grad_norm + NORM_EPS))

        states = {'d1': (master_down, mom_down, var_down, 0), 'd2': (master_down, mom_down, var_down, 1),
                  'u1': (master_up, mom_up, var_up, 0), 'u2': (master_up, mom_up, var_up, 1)}
        order = ('d2', 'u2', 'd1', 'u1')
        gathered = {}
        scale = clip_scale
        for name in order:
            master, mom, var, layer = states[name]
            near = pieces[name][0]
            cols = near.shape[1]
            cut = [lax.dynamic_slice(arr, (layer, 0, rep * cols), (1, near.shape[0], cols))[0] for arr in (master, mom, var)]
            mom_new, var_new = adam_parts(near, cut[1], cut[2], scale)
            half_new = adam_master(mom_new, var_new, cut[0]).astype(BF16)
            half_new, scale = lax.optimization_barrier((half_new, scale))
            from_x = swap_x(half_new)
            from_xy = swap_y(from_x)
            from_xc = swap_c(from_x)
            from_xyc = swap_c(from_xy)
            gathered[name] = (from_x, from_xc, from_xy, from_xyc)

        near_all, far_all = {}, {}
        for names in (('d1', 'd2'), ('u1', 'u2')):
            group = lax.optimization_barrier(([pieces[name][2:4] for name in names], scale))[0]
            for name, (near, far) in zip(names, group):
                near_all[name], far_all[name] = near, far

        def laid_grad(names, shape):
            grad = jnp.zeros(shape, F32)
            for layer, name in enumerate(names):
                spans, axis = pieces[name][4:]
                cols = shape[2] // 2
                for parts, side in ((near_all[name], rep), (far_all[name], 1 - rep)):
                    for part, span in zip(parts, spans):
                        start = (layer, 0, side * cols + span[0]) if axis else (layer, span[0], side * cols)
                        grad = lax.dynamic_update_slice(grad, part[None], start)
            return grad

        def full_update(grad, master, mom, var):
            mom_new, var_new = adam_parts(grad, mom, var, scale)
            master_new = adam_master(mom_new, var_new, master)
            return master_new, mom_new, var_new, master_new.astype(BF16)

        def assemble(names, shard, shape):
            rows = shard.shape[1]
            other = swap_c(shard)
            out = jnp.zeros(shape, BF16)
            out = lax.dynamic_update_slice(out, shard, (0, (2 * own_x + own_c) * rows, 0))
            out = lax.dynamic_update_slice(out, other, (0, (2 * own_x + 1 - own_c) * rows, 0))
            far_x = 2 * (1 - own_x)
            for name in order:
                if name not in names:
                    continue
                layer = states[name][3]
                from_x, from_xc, from_xy, from_xyc = gathered[name]
                cols = from_x.shape[1]
                out = lax.dynamic_update_slice(out, from_x[None], (layer, (far_x + own_c) * rows, rep * cols))
                out = lax.dynamic_update_slice(out, from_xc[None], (layer, (far_x + 1 - own_c) * rows, rep * cols))
                out = lax.dynamic_update_slice(out, from_xy[None], (layer, (far_x + own_c) * rows, (1 - rep) * cols))
                out = lax.dynamic_update_slice(out, from_xyc[None], (layer, (far_x + 1 - own_c) * rows, (1 - rep) * cols))
            return out

        grad_down = laid_grad(('d1', 'd2'), master_down.shape)
        grad_up = laid_grad(('u1', 'u2'), master_up.shape)
        master_down_new, mom_down_new, var_down_new, shard_down = lax.optimization_barrier(full_update(grad_down, master_down, mom_down, var_down))
        master_up_new, mom_up_new, var_up_new, shard_up = lax.optimization_barrier(full_update(grad_up, master_up, mom_up, var_up))
        w_down_new = assemble(('d1', 'd2'), shard_down, w_down.shape)
        w_up_new = assemble(('u1', 'u2'), shard_up, w_up.shape)
        return (w_up_new, w_down_new, master_up_new, master_down_new, mom_up_new, mom_down_new, var_up_new, var_down_new, grad_norm)


    return jax.shard_map(device_step, mesh=mesh, in_specs=(batch_spec, batch_spec, whole_spec, whole_spec, shard_spec, shard_spec, shard_spec, shard_spec, shard_spec, shard_spec, whole_spec), out_specs=(whole_spec, whole_spec, shard_spec, shard_spec, shard_spec, shard_spec, shard_spec, shard_spec, whole_spec), check_vma=False)
```

time: 3700 us -> 2390 us (0.65)
  waiting for transfers between devices: 2800 us -> 846 us
  matrix products: 377 us -> 856 us
  blocking collectives: 7.11 us -> 208 us
  local copies, waits for them, and re-layouts: 277 us -> 216 us
  starting transfers between devices: 0.29 us -> 45.3 us
    reduce_scatter x4 -> x0, waiting for transfers between devices: 1240 us -> none  [the longest x1 375 us: device_step(): lax.psum_scatter(grad_down2, 'data', scatter_dimension=0, tiled=True)]
    psum x1 -> x0, waiting for transfers between devices: 1140 us -> none  [device_step(): lax.psum(jnp.stack([shard_up1, shard_up2]), 'replica') / total_devices]
    ppermute x0 -> x60, waiting for transfers between devices: none -> 846 us  [the longest x14 566 us: swap_x(): return lax.ppermute(val, 'data', along_x)]
    dot_general x10 -> x73, matrix products: 377 us -> 856 us  [mul(): lax.dot_general(left, right, (((left_dim,), (right_dim,)), ((), ())), pre...]
    all_gather x2 -> x0, waiting for transfers between devices: 418 us -> none  [the longest x1 256 us: device_step(): lax.all_gather(master_down_new.astype(jnp.bfloat16), 'data', axis=1, tile...]
    unnamed x20 -> x103, local copies, waits for them, and re-layouts: 277 us -> 8.27 us
    psum x1, blocking collectives: 7.11 us -> 208 us  [device_step(): grad_norm = jnp.sqrt(lax.psum(local_sq, ('replica', 'data')))]
    dynamic_update_slice x0 -> x40, local copies, waits for them, and re-layouts: none -> 143 us  [the longest x20 58.3 us: laid_grad(): grad = lax.dynamic_update_slice(grad, part[None], start)]
  transfers between devices with their start and end apart: 7 -> 60, of which waited for: 7 -> 19; matrix products, arithmetic and copies ran while one was open for 14% -> 40% of each run, Pallas kernels for 0% -> 0%
where the time goes in v1:
time: 2390 us; the launch traced here: 2380 us
  matrix products  856 us (36%)
  waiting for transfers between devices  846 us (35%)
  local copies, waits for them, and re-layouts  216 us (9%)
  blocking collectives  208 us (9%)
  other arithmetic  200 us (8%)
  starting transfers between devices  45.3 us (2%)
    dot_general x73, matrix products, mul(): lax.dot_general(left, right, (((left_dim,), (right_dim,)), ((), ())), pre...  856 us
    ppermute x14, waiting for transfers between devices, swap_x(): return lax.ppermute(val, 'data', along_x)  566 us
    ppermute x16, waiting for transfers between devices, swap_y(): return lax.ppermute(val, 'replica', along_y)  280 us
    psum x1, blocking collectives, device_step(): grad_norm = jnp.sqrt(lax.psum(local_sq, ('replica', 'data')))  208 us
    convert_element_type x2, other arithmetic, full_update(): return (master_new, mom_new, var_new, master_new.astype(BF16))  138 us
    dynamic_update_slice x20, local copies, waits for them, and re-layouts, laid_grad(): grad = lax.dynamic_update_slice(grad, part[None], start)  58.3 us
    convert_element_type x4, other arithmetic, device_step(): half_new = adam_master(mom_new, var_new, cut[0]).astype(BF16)  51.5 us
  transfers between devices with their start and end apart: 60, of which 19 were waited for; matrix products, arithmetic and copies ran while one was open for 40% of the time, Pallas kernels for 0%

profile of v1, /device:TPU:0, one launch (start us, length us, event | category | flops | bytes accessed | tf_op | source)
XLA Modules:
  0.0 2381.8 jit_solution(2060744811467954910)
XLA Ops:
  7.8 39.9 %fusion.13 = (bf16[8960,1024]{1,0:T(8,128)(2,1)}, bf16[8960,1024]{1,0:T(8,128)(2,1)}) fusion(bf16[1024,1536]{1,0:T(8,128)(2,1)} %param.11, bf16[2,1536,8960]{2,1,0:T(8,128)(2,1)} %param.13), kind=kOutput, calls=%fused_computation.26 | convolution fusion | flops 28249948160 | bytes 67371008 | tf_op jit(solution)/shard_map/dot_general | solution.py:29
  48.4 35.4 %fusion.182 = bf16[1024,1536]{1,0:T(8,128)(2,1)} fusion(bf16[8960,1024]{1,0:T(8,128)(2,1)} %get-tuple-element.123, bf16[2,8960,1536]{2,1,0:T(8,128)(2,1)} %param.14), kind=kOutput, calls=%fused_computation.189 | convolution fusion | flops 28187295744 | bytes 49020928 | tf_op jit(solution)/shard_map/dot_general | solution.py:29
  83.9 40.0 %fusion.22 = (bf16[8960,1024]{1,0:T(8,128)(2,1)}, bf16[8960,1024]{1,0:T(8,128)(2,1)}) fusion(bf16[1024,1536]{1,0:T(8,128)(2,1)S(1)} %collective-permute-done, bf16[2,1536,8960]{2,1,0:T(8,128)(2,1)} %param.13), kind=kOutput, calls=%fused_computation.35 | convolution fusion | flops 28249948160 | bytes 67371008 | tf_op jit(solution)/shard_map/dot_general | solution.py:29
  123.9 35.7 %fusion.185 = bf16[1024,1536]{1,0:T(8,128)(2,1)} fusion(bf16[8960,1024]{1,0:T(8,128)(2,1)} %get-tuple-element.121, bf16[2,8960,1536]{2,1,0:T(8,128)(2,1)} %param.14), kind=kOutput, calls=%fused_computation.190 | convolution fusion | flops 28187295744 | bytes 49020928 | tf_op jit(solution)/shard_map/dot_general | solution.py:29
  161.9 80.0 %fusion.9 = (bf16[8960,2048]{0,1:T(8,128)(2,1)}, bf16[2048,8960]{1,0:T(8,128)(2,1)}) fusion(bf16[2,1536,8960]{2,1,0:T(8,128)(2,1)} %param.13, bf16[2048,1536]{1,0:T(8,128)(2,1)S(1)} %pad_maximum_fusion.5.clone.5), kind=kOutput, calls=%fused_computation.12 | convolution fusion | flops 56499896320 | bytes 107216896 | tf_op jit(solution)/shard_map/dot_general | solution.py:29
  246.7 96.7 %fusion.5 = bf16[8960,2048]{0,1:T(8,128)(2,1)} fusion(bf16[2048,8960]{1,0:T(8,128)(2,1)} %get-tuple-element.126, bf16[2048,1536]{1,0:T(8,128)(2,1)S(1)} %constant_dynamic-update-slice_fusion.4, bf16[2,8960,1536]{2,1,0:T(8,128)(2,1)} %param.14), kind=kOutput, calls=%fused_computation.6 | convolution fusion | flops 56609996800 | bytes 107216896 | tf_op jit(solution)/shard_map/dot_general | solution.py:29
  343.3 66.8 %fusion.63 = bf16[2048,1536]{1,0:T(8,128)(2,1)} fusion(bf16[8960,2048]{0,1:T(8,128)(2,1)} %fusion.5, bf16[2,1536,8960]{2,1,0:T(8,128)(2,1)} %param.13), kind=kOutput, calls=%fused_computation.84 | convolution fusion | flops 56374591488 | bytes 70516736 | tf_op jit(solution)/shard_map/dot_general | solution.py:29
  413.4 47.2 %fusion.18 = bf16[8960,1024]{1,0:T(8,128)(2,1)} fusion(bf16[8960,1024]{1,0:T(8,128)(2,1)} %get-tuple-element.124, bf16[1024,1536]{1,0:T(8,128)(2,1)S(1)} %get-tuple-element.61, bf16[2,8960,1536]{2,1,0:T(8,128)(2,1)} %param.14), kind=kOutput, calls=%fused_computation.31 | convolution fusion | flops 28304998400 | bytes 67371008 | tf_op jit(solution)/shard_map/dot_general | solution.py:29
  509.2 42.4 %fusion.27 = bf16[8960,1024]{1,0:T(8,128)(2,1)S(1)} fusion(bf16[8960,1024]{1,0:T(8,128)(2,1)} %get-tuple-element.122, bf16[1024,1536]{1,0:T(8,128)(2,1)S(1)} %get-tuple-element.62, bf16[2,8960,1536]{2,1,0:T(8,128)(2,1)} %param.14), kind=kOutput, calls=%fused_computation.40 | convolution fusion | flops 28304998400 | bytes 67371008 | tf_op jit(solution)/shard_map/dot_general | solution.py:29
  712.7 10.1 fusion.94
  732.4 10.0 fusion.98
  754.3 10.8 fusion.129
  794.7 12.3 collective-permute-done.22
  808.5 10.4 fusion.159
  818.9 26.0 %collective-permute-done.25 = f32[384,1152]{1,0:T(8,128)} collective-permute-done((f32[384,1152]{1,0:T(8,128)S(1)}, f32[384,1152]{1,0:T(8,128)}, u32[]{:S(2)}, u32[]{:S(2)}) %collective-permute-start.25) | collective-permute-done | bytes 1769504 | tf_op jit(solution)/shard_map/ppermute | solution.py:61
  846.4 36.4 %collective-permute-done.28 = f32[384,1152]{1,0:T(8,128)} collective-permute-done((f32[384,1152]{1,0:T(8,128)S(1)}, f32[384,1152]{1,0:T(8,128)}, u32[]{:S(2)}, u32[]{:S(2)}) %collective-permute-start.28) | collective-permute-done | bytes 1769504 | tf_op jit(solution)/shard_map/ppermute | solution.py:61
  909.4 10.8 fusion.141
  920.2 36.3 %collective-permute-done.16 = f32[1120,768]{1,0:T(8,128)} collective-permute-done((f32[1120,768]{1,0:T(8,128)}, f32[1120,768]{1,0:T(8,128)}, u32[]{:S(2)}, u32[]{:S(2)}) %collective-permute-start.16) | collective-permute-done | bytes 3440672 | tf_op jit(solution)/shard_map/ppermute | solution.py:61
  956.5 73.7 %collective-permute-done.19 = f32[1120,768]{1,0:T(8,128)} collective-permute-done((f32[1120,768]{1,0:T(8,128)}, f32[1120,768]{1,0:T(8,128)}, u32[]{:S(2)}, u32[]{:S(2)}) %collective-permute-start.19) | collective-permute-done | bytes 3440672 | tf_op jit(solution)/shard_map/ppermute | solution.py:61
  1040.4 63.6 %collective-permute-done.4 = f32[1120,768]{1,0:T(8,128)} collective-permute-done((f32[1120,768]{1,0:T(8,128)}, f32[1120,768]{1,0:T(8,128)}, u32[]{:S(2)}, u32[]{:S(2)}) %collective-permute-start.4) | collective-permute-done | bytes 3440672 | tf_op jit(solution)/shard_map/ppermute | solution.py:61
  1104.0 73.7 %collective-permute-done.7 = f32[1120,768]{1,0:T(8,128)} collective-permute-done((f32[1120,768]{1,0:T(8,128)}, f32[1120,768]{1,0:T(8,128)}, u32[]{:S(2)}, u32[]{:S(2)}) %collective-permute-start.7) | collective-permute-done | bytes 3440672 | tf_op jit(solution)/shard_map/ppermute | solution.py:61
  1179.3 10.2 multiply_reduce_fusion.4
  1200.1 12.7 multiply_reduce_fusion.3
  1215.2 38.3 %collective-permute-done.10 = f32[384,2304]{1,0:T(8,128)} collective-permute-done((f32[384,2304]{1,0:T(8,128)}, f32[384,2304]{1,0:T(8,128)}, u32[]{:S(2)}, u32[]{:S(2)}) %collective-permute-start.10) | collective-permute-done | bytes 3538976 | tf_op jit(solution)/shard_map/ppermute | solution.py:61
  1255.0 12.8 multiply_reduce_fusion
  1267.8 56.4 %collective-permute-done.13 = f32[384,2176]{1,0:T(8,128)} collective-permute-done((f32[384,2176]{1,0:T(8,128)}, f32[384,2176]{1,0:T(8,128)}, u32[]{:S(2)}, u32[]{:S(2)}) %collective-permute-start.13) | collective-permute-done | bytes 3342368 | tf_op jit(solution)/shard_map/ppermute | solution.py:61
  1325.7 10.9 multiply_reduce_fusion.5
  1338.5 207.6 %psum.7 = f32[]{:T(128)} all-reduce(f32[]{:T(128)S(6)} %add.388), channel_id=1, replica_groups=mesh['replica'=2,'data'=4] {'replica','data'}, use_global_device_ids=true, to_apply=%region_10.11 | all-reduce | flops 1 | bytes 8 | tf_op jit(solution)/shard_map/psum | solution.py:164
  1546.8 11.7 fusion.90
  1558.6 13.1 fusion.91
  1571.7 13.3 fusion.92
  1585.0 13.3 fusion.93
  1602.9 13.2 broadcast_in_dim.143
  1645.9 69.1 %fusion.407 = (bf16[2,2240,1536]{2,1,0:T(8,128)(2,1)}, f32[2,2240,1536]{2,1,0:T(8,128)}, f32[2,2240,1536]{2,1,0:T(8,128)}, f32[2,2240,1536]{2,1,0:T(8,128)}) fusion(f32[2,2240,1536]{2,1,0:T(8,128)} %param.16, f32[2,2240,1536]{2,1,0:T(8,128)} %bitcast_dynamic-update-slice_fusion.10, f32[]{:T(128)S(6)} %mul.378, f32[2,2240,1536]{2,1,0:T(8,128)} %param.18, ...), kind=kLoop, calls=%fused_computation.470 | loop fusion | flops 89456640 | bytes 206438400 | tf_op jit(solution)/shard_map/convert_element_type | solution.py:206
  1716.4 71.6 %collective-permute-done.37 = f32[384,2176]{1,0:T(8,128)} collective-permute-done((f32[384,2176]{1,0:T(8,128)}, f32[384,2176]{1,0:T(8,128)}, u32[]{:S(2)}, u32[]{:S(2)}) %collective-permute-start.37) | collective-permute-done | bytes 3342368 | tf_op jit(solution)/shard_map/ppermute | solution.py:67
  1788.1 74.0 %collective-permute-done.36 = f32[384,2304]{1,0:T(8,128)} collective-permute-done((f32[384,2304]{1,0:T(8,128)}, f32[384,2304]{1,0:T(8,128)}, u32[]{:S(2)}, u32[]{:S(2)}) %collective-permute-start.36) | collective-permute-done | bytes 3538976 | tf_op jit(solution)/shard_map/ppermute | solution.py:67
  1862.0 11.5 broadcast_in_dim.121
  1904.7 68.9 %fusion.408 = (bf16[2,384,8960]{2,1,0:T(8,128)(2,1)}, f32[2,384,8960]{2,1,0:T(8,128)}, f32[2,384,8960]{2,1,0:T(8,128)}, f32[2,384,8960]{2,1,0:T(8,128)}) fusion(f32[2,384,8960]{2,1,0:T(8,128)} %param.15, f32[2,384,8960]{2,1,0:T(8,128)} %bitcast_dynamic-update-slice_fusion.26, f32[]{:T(128)S(6)} %mul.378, f32[2,384,8960]{2,1,0:T(8,128)} %param.17, ...), kind=kLoop, calls=%fused_computation.471 | loop fusion | flops 89456640 | bytes 206438400 | tf_op jit(solution)/shard_map/convert_element_type | solution.py:206
  1977.4 17.5 broadcast_in_dim.142
  1995.0 13.9 constant_dynamic-update-slice_fusion.1
  2008.8 42.4 %collective-permute-done.56 = bf16[2240,768]{1,0:T(8,128)(2,1)} collective-permute-done((bf16[2240,768]{1,0:T(8,128)(2,1)}, bf16[2240,768]{1,0:T(8,128)(2,1)}, u32[]{:S(2)}, u32[]{:S(2)}) %collective-permute-start.56) | collective-permute-done | bytes 3440672 | tf_op jit(solution)/shard_map/ppermute | solution.py:61
  2051.2 17.5 broadcast_in_dim.120
  2074.8 49.6 %collective-permute-done.39 = bf16[384,4480]{1,0:T(8,128)(2,1)S(1)} collective-permute-done((bf16[384,4480]{1,0:T(8,128)(2,1)}, bf16[384,4480]{1,0:T(8,128)(2,1)S(1)}, u32[]{:S(2)}, u32[]{:S(2)}) %collective-permute-start.39) | collective-permute-done | bytes 3440672 | tf_op jit(solution)/shard_map/ppermute | solution.py:61
  2126.9 12.5 constant_dynamic-update-slice_fusion
  2149.8 50.5 %collective-permute-done.43 = bf16[384,4480]{1,0:T(8,128)(2,1)S(1)} collective-permute-done((bf16[384,4480]{1,0:T(8,128)(2,1)S(1)}, bf16[384,4480]{1,0:T(8,128)(2,1)S(1)}, u32[]{:S(2)}, u32[]{:S(2)}) %collective-permute-start.43) | collective-permute-done | bytes 3440672 | tf_op jit(solution)/shard_map/ppermute | solution.py:61
  2215.2 62.5 %collective-permute-done.41 = bf16[384,4480]{1,0:T(8,128)(2,1)S(1)} collective-permute-done((bf16[384,4480]{1,0:T(8,128)(2,1)S(1)}, bf16[384,4480]{1,0:T(8,128)(2,1)S(1)}, u32[]{:S(2)}, u32[]{:S(2)}) %collective-permute-start.41) | collective-permute-done | bytes 3440672 | tf_op jit(solution)/shard_map/ppermute | solution.py:67
  2277.6 71.8 %collective-permute-done.45 = bf16[384,4480]{1,0:T(8,128)(2,1)S(1)} collective-permute-done((bf16[384,4480]{1,0:T(8,128)(2,1)S(1)}, bf16[384,4480]{1,0:T(8,128)(2,1)S(1)}, u32[]{:S(2)}, u32[]{:S(2)}) %collective-permute-start.45) | collective-permute-done | bytes 3440672 | tf_op jit(solution)/shard_map/ppermute | solution.py:67
  2352.0 12.5 constant_dynamic-update-slice_fusion.2
  (307 shorter events, 453.9 us)
Async XLA Ops:
  0.6 83.3 %collective-permute-start = (bf16[1024,1536]{1,0:T(8,128)(2,1)}, bf16[1024,1536]{1,0:T(8,128)(2,1)S(1)}, u32[]{:S(2)}, u32[]{:S(2)}) collective-permute-start(bf16[1024,1536]{1,0:T(8,128)(2,1)} %param.11), channel_id=1, source_target_pairs={{0,4},{4,0},{1,5},{5,1},{2,6},{6,2},{3,7},{7,3}} | collective-permute-start | bytes 9437192 | tf_op jit(solution)/shard_map/ppermute | solution.py:67
  4.0 237.9 %collective-permute-start.1 = (bf16[1024,1536]{1,0:T(8,128)(2,1)}, bf16[1024,1536]{1,0:T(8,128)(2,1)}, u32[]{:S(2)}, u32[]{:S(2)}) collective-permute-start(bf16[1024,1536]{1,0:T(8,128)(2,1)} %param.12), channel_id=1, source_target_pairs={{0,4},{4,0},{1,5},{5,1},{2,6},{6,2},{3,7},{7,3}} | collective-permute-start | bytes 9437192 | tf_op jit(solution)/shard_map/ppermute | solution.py:67
  555.9 104.8 %collective-permute-start.23 = (f32[384,1152]{1,0:T(8,128)}, f32[384,1152]{1,0:T(8,128)}, u32[]{:S(2)}, u32[]{:S(2)}) collective-permute-start(f32[384,1152]{1,0:T(8,128)} %convolution_add_fusion.14), channel_id=1, source_target_pairs={{0,1},{1,0},{2,3},{3,2},{4,5},{5,4},{6,7},{7,6}} | collective-permute-start | bytes 5308424 | tf_op jit(solution)/shard_map/ppermute | solution.py:64
  558.5 102.6 %collective-permute-start.20 = (f32[384,1152]{1,0:T(8,128)}, f32[384,1152]{1,0:T(8,128)}, u32[]{:S(2)}, u32[]{:S(2)}) collective-permute-start(f32[384,1152]{1,0:T(8,128)} %convolution_add_fusion.18), channel_id=1, source_target_pairs={{0,1},{1,0},{2,3},{3,2},{4,5},{5,4},{6,7},{7,6}} | collective-permute-start | bytes 5308424 | tf_op jit(solution)/shard_map/ppermute | solution.py:64
  561.5 117.2 %collective-permute-start.21 = (f32[384,1152]{1,0:T(8,128)}, f32[384,1152]{1,0:T(8,128)S(1)}, u32[]{:S(2)}, u32[]{:S(2)}) collective-permute-start(f32[384,1152]{1,0:T(8,128)} %convolution_add_fusion.16), channel_id=1, source_target_pairs={{0,1},{1,0},{2,3},{3,2},{4,5},{5,4},{6,7},{7,6}} | collective-permute-start | bytes 5308424 | tf_op jit(solution)/shard_map/ppermute | solution.py:64
  562.6 83.9 %collective-permute-start.29 = (f32[384,1024]{1,0:T(8,128)S(1)}, f32[384,1024]{1,0:T(8,128)}, u32[]{:S(2)}, u32[]{:S(2)}) collective-permute-start(f32[384,1024]{1,0:T(8,128)S(1)} %convolution_add_fusion.21), channel_id=1, source_target_pairs={{0,1},{1,0},{2,3},{3,2},{4,5},{5,4},{6,7},{7,6}} | collective-permute-start | bytes 4718600 | tf_op jit(solution)/shard_map/ppermute | solution.py:64
  565.4 95.3 %collective-permute-start.30 = (f32[384,1024]{1,0:T(8,128)}, f32[384,1024]{1,0:T(8,128)}, u32[]{:S(2)}, u32[]{:S(2)}) collective-permute-start(f32[384,1024]{1,0:T(8,128)} %convolution_add_fusion.20), channel_id=1, source_target_pairs={{0,1},{1,0},{2,3},{3,2},{4,5},{5,4},{6,7},{7,6}} | collective-permute-start | bytes 4718600 | tf_op jit(solution)/shard_map/ppermute | solution.py:64
  660.7 69.5 %collective-permute-start.17 = (f32[1120,768]{1,0:T(8,128)}, f32[1120,768]{1,0:T(8,128)}, u32[]{:S(2)}, u32[]{:S(2)}) collective-permute-start(f32[1120,768]{1,0:T(8,128)} %convolution_add_fusion.2), channel_id=1, source_target_pairs={{0,1},{1,0},{2,3},{3,2},{4,5},{5,4},{6,7},{7,6}} | collective-permute-start | bytes 10321928 | tf_op jit(solution)/shard_map/ppermute | solution.py:64
  661.2 68.5 %collective-permute-start.12 = (f32[384,2176]{1,0:T(8,128)}, f32[384,2176]{1,0:T(8,128)}, u32[]{:S(2)}, u32[]{:S(2)}) collective-permute-start(f32[384,2176]{1,0:T(8,128)} %fusion.102), channel_id=1, source_target_pairs={{0,1},{1,0},{2,3},{3,2},{4,5},{5,4},{6,7},{7,6}} | collective-permute-start | bytes 10027016 | tf_op jit(solution)/shard_map/ppermute | solution.py:64
  682.8 64.3 %collective-permute-start.14 = (f32[1120,768]{1,0:T(8,128)}, f32[1120,768]{1,0:T(8,128)}, u32[]{:S(2)}, u32[]{:S(2)}) collective-permute-start(f32[1120,768]{1,0:T(8,128)} %convolution_add_fusion.6), channel_id=1, source_target_pairs={{0,1},{1,0},{2,3},{3,2},{4,5},{5,4},{6,7},{7,6}} | collective-permute-start | bytes 10321928 | tf_op jit(solution)/shard_map/ppermute | solution.py:64
  774.9 134.5 %collective-permute-start.9 = (f32[384,2304]{1,0:T(8,128)}, f32[384,2304]{1,0:T(8,128)}, u32[]{:S(2)}, u32[]{:S(2)}) collective-permute-start(f32[384,2304]{1,0:T(8,128)} %fusion.94), channel_id=1, source_target_pairs={{0,1},{1,0},{2,3},{3,2},{4,5},{5,4},{6,7},{7,6}} | collective-permute-start | bytes 10616840 | tf_op jit(solution)/shard_map/ppermute | solution.py:64
  774.9 69.9 %collective-permute-start.25 = (f32[384,1152]{1,0:T(8,128)S(1)}, f32[384,1152]{1,0:T(8,128)}, u32[]{:S(2)}, u32[]{:S(2)}) collective-permute-start(f32[384,1152]{1,0:T(8,128)S(1)} %copy-done.28), channel_id=1, source_target_pairs={{0,2},{1,3},{2,0},{3,1},{4,6},{5,7},{6,4},{7,5}} | collective-permute-start | bytes 5308424 | tf_op jit(solution)/shard_map/ppermute | solution.py:61
  775.3 107.5 %collective-permute-start.28 = (f32[384,1152]{1,0:T(8,128)S(1)}, f32[384,1152]{1,0:T(8,128)}, u32[]{:S(2)}, u32[]{:S(2)}) collective-permute-start(f32[384,1152]{1,0:T(8,128)S(1)} %copy-done.27), channel_id=1, source_target_pairs={{0,2},{1,3},{2,0},{3,1},{4,6},{5,7},{6,4},{7,5}} | collective-permute-start | bytes 5308424 | tf_op jit(solution)/shard_map/ppermute | solution.py:61
  794.3 162.2 %collective-permute-start.16 = (f32[1120,768]{1,0:T(8,128)}, f32[1120,768]{1,0:T(8,128)}, u32[]{:S(2)}, u32[]{:S(2)}) collective-permute-start(f32[1120,768]{1,0:T(8,128)} %fusion.177), channel_id=1, source_target_pairs={{0,2},{1,3},{2,0},{3,1},{4,6},{5,7},{6,4},{7,5}} | collective-permute-start | bytes 10321928 | tf_op jit(solution)/shard_map/ppermute | solution.py:61
  806.9 223.3 %collective-permute-start.19 = (f32[1120,768]{1,0:T(8,128)}, f32[1120,768]{1,0:T(8,128)}, u32[]{:S(2)}, u32[]{:S(2)}) collective-permute-start(f32[1120,768]{1,0:T(8,128)} %fusion.181), channel_id=1, source_target_pairs={{0,2},{1,3},{2,0},{3,1},{4,6},{5,7},{6,4},{7,5}} | collective-permute-start | bytes 10321928 | tf_op jit(solution)/shard_map/ppermute | solution.py:61
  844.9 259.1 %collective-permute-start.4 = (f32[1120,768]{1,0:T(8,128)}, f32[1120,768]{1,0:T(8,128)}, u32[]{:S(2)}, u32[]{:S(2)}) collective-permute-start(f32[1120,768]{1,0:T(8,128)} %fusion.153), channel_id=1, source_target_pairs={{0,2},{1,3},{2,0},{3,1},{4,6},{5,7},{6,4},{7,5}} | collective-permute-start | bytes 10321928 | tf_op jit(solution)/shard_map/ppermute | solution.py:61
  882.8 294.9 %collective-permute-start.7 = (f32[1120,768]{1,0:T(8,128)}, f32[1120,768]{1,0:T(8,128)}, u32[]{:S(2)}, u32[]{:S(2)}) collective-permute-start(f32[1120,768]{1,0:T(8,128)} %fusion.159), channel_id=1, source_target_pairs={{0,2},{1,3},{2,0},{3,1},{4,6},{5,7},{6,4},{7,5}} | collective-permute-start | bytes 10321928 | tf_op jit(solution)/shard_map/ppermute | solution.py:61
  909.4 289.8 %collective-permute-start.5 = (f32[1120,768]{1,0:T(8,128)}, f32[1120,768]{1,0:T(8,128)}, u32[]{:S(2)}, u32[]{:S(2)}) collective-permute-start(f32[1120,768]{1,0:T(8,128)} %fusion.114), channel_id=1, source_target_pairs={{0,1},{1,0},{2,3},{3,2},{4,5},{5,4},{6,7},{7,6}} | collective-permute-start | bytes 10321928 | tf_op jit(solution)/shard_map/ppermute | solution.py:64
  956.5 257.6 %collective-permute-start.8 = (f32[384,2304]{1,0:T(8,128)}, f32[384,2304]{1,0:T(8,128)}, u32[]{:S(2)}, u32[]{:S(2)}) collective-permute-start(f32[384,2304]{1,0:T(8,128)} %fusion.98), channel_id=1, source_target_pairs={{0,1},{1,0},{2,3},{3,2},{4,5},{5,4},{6,7},{7,6}} | collective-permute-start | bytes 10616840 | tf_op jit(solution)/shard_map/ppermute | solution.py:64
  1030.2 223.3 %collective-permute-start.10 = (f32[384,2304]{1,0:T(8,128)}, f32[384,2304]{1,0:T(8,128)}, u32[]{:S(2)}, u32[]{:S(2)}) collective-permute-start(f32[384,2304]{1,0:T(8,128)} %fusion.141), channel_id=1, source_target_pairs={{0,2},{1,3},{2,0},{3,1},{4,6},{5,7},{6,4},{7,5}} | collective-permute-start | bytes 10616840 | tf_op jit(solution)/shard_map/ppermute | solution.py:61
  1104.0 221.7 %collective-permute-start.11 = (f32[384,2176]{1,0:T(8,128)}, f32[384,2176]{1,0:T(8,128)}, u32[]{:S(2)}, u32[]{:S(2)}) collective-permute-start(f32[384,2176]{1,0:T(8,128)} %fusion.106), channel_id=1, source_target_pairs={{0,1},{1,0},{2,3},{3,2},{4,5},{5,4},{6,7},{7,6}} | collective-permute-start | bytes 10027016 | tf_op jit(solution)/shard_map/ppermute | solution.py:64
  1177.7 146.5 %collective-permute-start.13 = (f32[384,2176]{1,0:T(8,128)}, f32[384,2176]{1,0:T(8,128)}, u32[]{:S(2)}, u32[]{:S(2)}) collective-permute-start(f32[384,2176]{1,0:T(8,128)} %fusion.129), channel_id=1, source_target_pairs={{0,2},{1,3},{2,0},{3,1},{4,6},{5,7},{6,4},{7,5}} | collective-permute-start | bytes 10027016 | tf_op jit(solution)/shard_map/ppermute | solution.py:61
  1199.1 444.8 %collective-permute-start.35 = (f32[384,1024]{1,0:T(8,128)}, f32[384,1024]{1,0:T(8,128)}, u32[]{:S(2)}, u32[]{:S(2)}) collective-permute-start(f32[384,1024]{1,0:T(8,128)} %get-tuple-element.80), channel_id=1, source_target_pairs={{0,4},{4,0},{1,5},{5,1},{2,6},{6,2},{3,7},{7,3}} | collective-permute-start | bytes 4718600 | tf_op jit(solution)/shard_map/ppermute | solution.py:67
  1214.1 386.7 %collective-permute-start.49 = (f32[1120,768]{1,0:T(8,128)S(1)}, f32[1120,768]{1,0:T(8,128)}, u32[]{:S(2)}, u32[]{:S(2)}) collective-permute-start(f32[1120,768]{1,0:T(8,128)S(1)} %get-tuple-element.96), channel_id=1, source_target_pairs={{0,4},{4,0},{1,5},{5,1},{2,6},{6,2},{3,7},{7,3}} | collective-permute-start | bytes 10321928 | tf_op jit(solution)/shard_map/ppermute | solution.py:67
  1253.5 349.3 %collective-permute-start.47 = (f32[1120,768]{1,0:T(8,128)}, f32[1120,768]{1,0:T(8,128)}, u32[]{:S(2)}, u32[]{:S(2)}) collective-permute-start(f32[1120,768]{1,0:T(8,128)} %get-tuple-element.92), channel_id=1, source_target_pairs={{0,4},{4,0},{1,5},{5,1},{2,6},{6,2},{3,7},{7,3}} | collective-permute-start | bytes 10321928 | tf_op jit(solution)/shard_map/ppermute | solution.py:67
  1324.2 274.1 %collective-permute-start.50 = (f32[1120,768]{1,0:T(8,128)}, f32[1120,768]{1,0:T(8,128)}, u32[]{:S(2)}, u32[]{:S(2)}) collective-permute-start(f32[1120,768]{1,0:T(8,128)} %get-tuple-element.97), channel_id=1, source_target_pairs={{0,4},{4,0},{1,5},{5,1},{2,6},{6,2},{3,7},{7,3}} | collective-permute-start | bytes 10321928 | tf_op jit(solution)/shard_map/ppermute | solution.py:67
  1337.9 263.0 %collective-permute-start.48 = (f32[1120,768]{1,0:T(8,128)}, f32[1120,768]{1,0:T(8,128)}, u32[]{:S(2)}, u32[]{:S(2)}) collective-permute-start(f32[1120,768]{1,0:T(8,128)} %get-tuple-element.93), channel_id=1, source_target_pairs={{0,4},{4,0},{1,5},{5,1},{2,6},{6,2},{3,7},{7,3}} | collective-permute-start | bytes 10321928 | tf_op jit(solution)/shard_map/ppermute | solution.py:67
  1598.3 116.7 %collective-permute-start.34 = (f32[384,1152]{1,0:T(8,128)}, f32[384,1152]{1,0:T(8,128)}, u32[]{:S(2)}, u32[]{:S(2)}) collective-permute-start(f32[384,1152]{1,0:T(8,128)} %get-tuple-element.79), channel_id=1, source_target_pairs={{0,4},{4,0},{1,5},{5,1},{2,6},{6,2},{3,7},{7,3}} | collective-permute-start | bytes 5308424 | tf_op jit(solution)/shard_map/ppermute | solution.py:67
  1600.8 115.5 %collective-permute-start.33 = (f32[384,1152]{1,0:T(8,128)}, f32[384,1152]{1,0:T(8,128)}, u32[]{:S(2)}, u32[]{:S(2)}) collective-permute-start(f32[384,1152]{1,0:T(8,128)} %get-tuple-element.78), channel_id=1, source_target_pairs={{0,4},{4,0},{1,5},{5,1},{2,6},{6,2},{3,7},{7,3}} | collective-permute-start | bytes 5308424 | tf_op jit(solution)/shard_map/ppermute | solution.py:67
  1600.9 115.6 %collective-permute-start.32 = (f32[384,1152]{1,0:T(8,128)}, f32[384,1152]{1,0:T(8,128)}, u32[]{:S(2)}, u32[]{:S(2)}) collective-permute-start(f32[384,1152]{1,0:T(8,128)} %get-tuple-element.77), channel_id=1, source_target_pairs={{0,4},{4,0},{1,5},{5,1},{2,6},{6,2},{3,7},{7,3}} | collective-permute-start | bytes 5308424 | tf_op jit(solution)/shard_map/ppermute | solution.py:67
  1602.8 185.2 %collective-permute-start.37 = (f32[384,2176]{1,0:T(8,128)}, f32[384,2176]{1,0:T(8,128)}, u32[]{:S(2)}, u32[]{:S(2)}) collective-permute-start(f32[384,2176]{1,0:T(8,128)} %get-tuple-element.86), channel_id=1, source_target_pairs={{0,4},{4,0},{1,5},{5,1},{2,6},{6,2},{3,7},{7,3}} | collective-permute-start | bytes 10027016 | tf_op jit(solution)/shard_map/ppermute | solution.py:67
  1644.0 218.1 %collective-permute-start.36 = (f32[384,2304]{1,0:T(8,128)}, f32[384,2304]{1,0:T(8,128)}, u32[]{:S(2)}, u32[]{:S(2)}) collective-permute-start(f32[384,2304]{1,0:T(8,128)} %get-tuple-element.85), channel_id=1, source_target_pairs={{0,4},{4,0},{1,5},{5,1},{2,6},{6,2},{3,7},{7,3}} | collective-permute-start | bytes 10616840 | tf_op jit(solution)/shard_map/ppermute | solution.py:67
  1715.0 260.6 %collective-permute-start.52 = (bf16[2240,768]{1,0:T(8,128)(2,1)}, bf16[2240,768]{1,0:T(8,128)(2,1)}, u32[]{:S(2)}, u32[]{:S(2)}) collective-permute-start(bf16[2240,768]{1,0:T(8,128)(2,1)} %fusion.90), channel_id=1, source_target_pairs={{0,2},{1,3},{2,0},{3,1},{4,6},{5,7},{6,4},{7,5}} | collective-permute-start | bytes 10321928 | tf_op jit(solution)/shard_map/ppermute | solution.py:61
  1716.3 410.6 %collective-permute-start.51 = (bf16[2,2240,1536]{2,1,0:T(8,128)(2,1)}, bf16[2,2240,1536]{2,1,0:T(8,128)(2,1)}, u32[]{:S(2)}, u32[]{:S(2)}) collective-permute-start(bf16[2,2240,1536]{2,1,0:T(8,128)(2,1)} %get-tuple-element.100), channel_id=1, source_target_pairs={{0,1},{1,0},{2,3},{3,2},{4,5},{5,4},{6,7},{7,6}} | collective-permute-start | bytes 41287688 | tf_op jit(solution)/shard_map/ppermute | solution.py:64
  1973.6 378.4 %collective-permute-start.38 = (bf16[2,384,8960]{2,1,0:T(8,128)(2,1)}, bf16[2,384,8960]{2,1,0:T(8,128)(2,1)}, u32[]{:S(2)}, u32[]{:S(2)}) collective-permute-start(bf16[2,384,8960]{2,1,0:T(8,128)(2,1)} %get-tuple-element.89), channel_id=1, source_target_pairs={{0,1},{1,0},{2,3},{3,2},{4,5},{5,4},{6,7},{7,6}} | collective-permute-start | bytes 41287688 | tf_op jit(solution)/shard_map/ppermute | solution.py:64
  1973.6 77.6 %collective-permute-start.56 = (bf16[2240,768]{1,0:T(8,128)(2,1)}, bf16[2240,768]{1,0:T(8,128)(2,1)}, u32[]{:S(2)}, u32[]{:S(2)}) collective-permute-start(bf16[2240,768]{1,0:T(8,128)(2,1)} %fusion.92), channel_id=1, source_target_pairs={{0,2},{1,3},{2,0},{3,1},{4,6},{5,7},{6,4},{7,5}} | collective-permute-start | bytes 10321928 | tf_op jit(solution)/shard_map/ppermute | solution.py:61
  1975.4 149.0 %collective-permute-start.39 = (bf16[384,4480]{1,0:T(8,128)(2,1)}, bf16[384,4480]{1,0:T(8,128)(2,1)S(1)}, u32[]{:S(2)}, u32[]{:S(2)}) collective-permute-start(bf16[384,4480]{1,0:T(8,128)(2,1)} %fusion.91), channel_id=1, source_target_pairs={{0,2},{1,3},{2,0},{3,1},{4,6},{5,7},{6,4},{7,5}} | collective-permute-start | bytes 10321928 | tf_op jit(solution)/shard_map/ppermute | solution.py:61
  1975.7 150.5 %collective-permute-start.54 = (bf16[2240,768]{1,0:T(8,128)(2,1)}, bf16[2240,768]{1,0:T(8,128)(2,1)}, u32[]{:S(2)}, u32[]{:S(2)}) collective-permute-start(bf16[2240,768]{1,0:T(8,128)(2,1)} %collective-permute-done.52), channel_id=1, source_target_pairs={{0,4},{4,0},{1,5},{5,1},{2,6},{6,2},{3,7},{7,3}} | collective-permute-start | bytes 10321928 | tf_op jit(solution)/shard_map/ppermute | solution.py:67
  2051.2 92.2 %collective-permute-start.53 = (bf16[2240,768]{1,0:T(8,128)(2,1)}, bf16[2240,768]{1,0:T(8,128)(2,1)S(1)}, u32[]{:S(2)}, u32[]{:S(2)}) collective-permute-start(bf16[2240,768]{1,0:T(8,128)(2,1)} %collective-permute-done.52), channel_id=1, source_target_pairs={{0,1},{1,0},{2,3},{3,2},{4,5},{5,4},{6,7},{7,6}} | collective-permute-start | bytes 10321928 | tf_op jit(solution)/shard_map/ppermute | solution.py:64
  2124.4 76.0 %collective-permute-start.43 = (bf16[384,4480]{1,0:T(8,128)(2,1)S(1)}, bf16[384,4480]{1,0:T(8,128)(2,1)S(1)}, u32[]{:S(2)}, u32[]{:S(2)}) collective-permute-start(bf16[384,4480]{1,0:T(8,128)(2,1)S(1)} %copy-done.10), channel_id=1, source_target_pairs={{0,2},{1,3},{2,0},{3,1},{4,6},{5,7},{6,4},{7,5}} | collective-permute-start | bytes 10321928 | tf_op jit(solution)/shard_map/ppermute | solution.py:61
  2126.1 76.2 %collective-permute-start.58 = (bf16[2240,768]{1,0:T(8,128)(2,1)}, bf16[2240,768]{1,0:T(8,128)(2,1)S(1)}, u32[]{:S(2)}, u32[]{:S(2)}) collective-permute-start(bf16[2240,768]{1,0:T(8,128)(2,1)} %collective-permute-done.56), channel_id=1, source_target_pairs={{0,4},{4,0},{1,5},{5,1},{2,6},{6,2},{3,7},{7,3}} | collective-permute-start | bytes 10321928 | tf_op jit(solution)/shard_map/ppermute | solution.py:67
  2126.9 75.9 %collective-permute-start.55 = (bf16[2240,768]{1,0:T(8,128)(2,1)}, bf16[2240,768]{1,0:T(8,128)(2,1)S(1)}, u32[]{:S(2)}, u32[]{:S(2)}) collective-permute-start(bf16[2240,768]{1,0:T(8,128)(2,1)} %collective-permute-done.54), channel_id=1, source_target_pairs={{0,1},{1,0},{2,3},{3,2},{4,5},{5,4},{6,7},{7,6}} | collective-permute-start | bytes 10321928 | tf_op jit(solution)/shard_map/ppermute | solution.py:64
  2143.4 65.3 %collective-permute-start.57 = (bf16[2240,768]{1,0:T(8,128)(2,1)}, bf16[2240,768]{1,0:T(8,128)(2,1)}, u32[]{:S(2)}, u32[]{:S(2)}) collective-permute-start(bf16[2240,768]{1,0:T(8,128)(2,1)} %collective-permute-done.56), channel_id=1, source_target_pairs={{0,1},{1,0},{2,3},{3,2},{4,5},{5,4},{6,7},{7,6}} | collective-permute-start | bytes 10321928 | tf_op jit(solution)/shard_map/ppermute | solution.py:64
  2200.3 77.3 %collective-permute-start.41 = (bf16[384,4480]{1,0:T(8,128)(2,1)S(1)}, bf16[384,4480]{1,0:T(8,128)(2,1)S(1)}, u32[]{:S(2)}, u32[]{:S(2)}) collective-permute-start(bf16[384,4480]{1,0:T(8,128)(2,1)S(1)} %collective-permute-done.39), channel_id=1, source_target_pairs={{0,4},{4,0},{1,5},{5,1},{2,6},{6,2},{3,7},{7,3}} | collective-permute-start | bytes 10321928 | tf_op jit(solution)/shard_map/ppermute | solution.py:67
  2202.3 147.2 %collective-permute-start.45 = (bf16[384,4480]{1,0:T(8,128)(2,1)S(1)}, bf16[384,4480]{1,0:T(8,128)(2,1)S(1)}, u32[]{:S(2)}, u32[]{:S(2)}) collective-permute-start(bf16[384,4480]{1,0:T(8,128)(2,1)S(1)} %collective-permute-done.43), channel_id=1, source_target_pairs={{0,4},{4,0},{1,5},{5,1},{2,6},{6,2},{3,7},{7,3}} | collective-permute-start | bytes 10321928 | tf_op jit(solution)/shard_map/ppermute | solution.py:67
  2202.8 146.7 %collective-permute-start.59 = (bf16[2240,768]{1,0:T(8,128)(2,1)S(1)}, bf16[2240,768]{1,0:T(8,128)(2,1)S(1)}, u32[]{:S(2)}, u32[]{:S(2)}) collective-permute-start(bf16[2240,768]{1,0:T(8,128)(2,1)S(1)} %collective-permute-done.58), channel_id=1, source_target_pairs={{0,1},{1,0},{2,3},{3,2},{4,5},{5,4},{6,7},{7,6}} | collective-permute-start | bytes 10321928 | tf_op jit(solution)/shard_map/ppermute | solution.py:64
  2208.7 157.8 %collective-permute-start.40 = (bf16[384,4480]{1,0:T(8,128)(2,1)S(1)}, bf16[384,4480]{1,0:T(8,128)(2,1)S(1)}, u32[]{:S(2)}, u32[]{:S(2)}) collective-permute-start(bf16[384,4480]{1,0:T(8,128)(2,1)S(1)} %collective-permute-done.39), channel_id=1, source_target_pairs={{0,1},{1,0},{2,3},{3,2},{4,5},{5,4},{6,7},{7,6}} | collective-permute-start | bytes 10321928 | tf_op jit(solution)/shard_map/ppermute | solution.py:64
  2277.6 96.8 %collective-permute-start.44 = (bf16[384,4480]{1,0:T(8,128)(2,1)S(1)}, bf16[384,4480]{1,0:T(8,128)(2,1)S(1)}, u32[]{:S(2)}, u32[]{:S(2)}) collective-permute-start(bf16[384,4480]{1,0:T(8,128)(2,1)S(1)} %collective-permute-done.43), channel_id=1, source_target_pairs={{0,1},{1,0},{2,3},{3,2},{4,5},{5,4},{6,7},{7,6}} | collective-permute-start | bytes 10321928 | tf_op jit(solution)/shard_map/ppermute | solution.py:64
  (63 other events, 2961.5 us)
